TPU v7x, 256 devices: a whole 4x4x8 slice. The times are simulated.
256 devices in a mesh: gy: 8 (over y, x_hi), gx: 32 (over x_lo, z, core).
Axes of the slice: x: 4 (x_hi: 2, x_lo: 2; x = x_hi * 2 + x_lo), y: 4, z: 8, core: 2. Of those that a mesh axis runs over, the one named last changes fastest.
Arguments:
- u_field: float32 [8, 2048, 2048], P(None, 'gx', 'gy')
- v_field: float32 [8, 2048, 2048], P(None, 'gx', 'gy')
- w_field: float32 [8, 2048, 2048], P(None, 'gx', 'gy')
- sep_x: int32 [16], replicated, may hold values from 1 to 128, as said below
- sep_y: int32 [16], replicated, may hold values from 1 to 256, as said below
- sep_z: int32 [16], replicated, may hold values from 1 to 4
Outputs:
- correlation: float32 [3, 16], replicated
Inputs may be any that keep to these rules, and one draw needn't show every extreme that they name: `sep_x`: every separation along x lies in 1 to 128, and 128 is among them in every draw; repeats may occur. `sep_y`: every separation along y lies in 1 to 256, and 256 is among them in every draw; repeats may occur.
All inputs are finite; a program needn't handle non-finite values.
Results may differ from a plain program's by a relative error of at most 0.0003.
Values sent between devices are 32-bit elements; how exact they have to be, the bound alone decides.
A program may use at most 64 MiB of HBM per device.

v0:
```python
import jax
import jax.numpy as jnp
from jax import lax
from jax.sharding import Mesh
from jax.sharding import PartitionSpec as P

GX = ("gx_0", "gx_1", "gx_2")
GY = ("gy_0", "gy_1")
GY_GX = ("gy_0", "gy_1", "gx_0", "gx_1", "gx_2")


def from_behind(value, axis, steps):
    count = lax.axis_size(axis)
    pairs = [(source, (source + steps) % count) for source in range(count)]
    return lax.ppermute(value, axis, pairs)


def by_axis(x, axes):
    for axis in axes:
        x = lax.psum(x, axis)
    return x


def lag_sums(widened, leading, lag_values, length, axis_dim):

    def one_lag(lag_entry):
        offset, lag_value = lag_entry
        head = lax.dynamic_slice_in_dim(widened, offset, length, axis_dim)
        tail = lax.dynamic_slice_in_dim(widened, offset + lag_value, length, axis_dim)
        return jnp.sum(head * tail)

    return lax.map(one_lag, (leading, lag_values))


def local(u_field, v_field, w_field, sep_x, sep_y, sep_z):
    planes, width_x, width_y = u_field.shape
    u_next = from_behind(u_field, GX, -1)
    u_after = from_behind(u_next, GX, -1)
    wide_x = jnp.concatenate([u_field, u_next, u_after], axis=1)
    v_next = from_behind(v_field, GY, -1)
    wide_y = jnp.concatenate([v_field, v_next], axis=2)
    offset_x = jnp.zeros_like(sep_x)
    offset_y = jnp.zeros_like(sep_y)
    sums_x = lag_sums(wide_x, offset_x, sep_x, width_x, 1)
    sums_y = lag_sums(wide_y, offset_y, sep_y, width_y, 2)
    padded = jnp.concatenate([w_field, jnp.zeros_like(w_field)], axis=0)

    def along_z(lag_value):
        shifted = lax.dynamic_slice_in_dim(padded, lag_value, planes, 0)
        return jnp.sum(w_field * shifted)

    sums_z = lax.map(along_z, sep_z)
    products = jnp.stack([sums_x, sums_y, sums_z], axis=0)
    squares = jnp.stack(
        [jnp.sum(u_field * u_field), jnp.sum(v_field * v_field), jnp.sum(w_field * w_field)]
    )
    totals, energy = (by_axis(products, GY_GX), by_axis(squares, GY_GX))
    factor = jnp.float32(planes) / (jnp.float32(planes) - sep_z.astype(jnp.float32))
    row_x = totals[0] / energy[0]
    row_y = totals[1] / energy[1]
    row_z = totals[2] / energy[2] * factor
    return jnp.stack([row_x, row_y, row_z], axis=0)


def solution(mesh):
    finer = Mesh(mesh.devices.reshape(4, 2, 2, 8, 2), ("gy_0", "gy_1", "gx_0", "gx_1", "gx_2"))
    placed = (P(None, GX, GY), P(None, GX, GY), P(None, GX, GY), P(), P(), P())
    return jax.shard_map(local, mesh=finer, in_specs=placed, out_specs=P(), check_vma=False)
```

profile of v0, /device:TPU:1, one launch (start us, length us, event | category | flops | bytes accessed | tf_op | source)
XLA Modules:
  0.0 266.0 jit_solution(17516855033638149033)
XLA Ops:
  0.0 3.2 %collective-permute-start = (f32[8,64,256]{2,1,0:T(8,128)}, f32[8,64,256]{2,1,0:T(8,128)S(1)}, u32[]{:S(2)}, u32[]{:S(2)}) collective-permute-start(f32[8,64,256]{2,1,0:T(8,128)} %param.12), channel_id=1, source_target_pairs={{0,31},{1,0},{2,1},{3,2},{4,3},{5,4},{6,5},{7,6},{8,7},{9,8},{10,9... | collective-permute-start | bytes 1572872 | tf_op jit(solution)/shard_map/ppermute | solution.py:15
  3.2 3.5 %collective-permute-start.2 = (f32[8,64,256]{2,1,0:T(8,128)}, f32[8,64,256]{2,1,0:T(8,128)}, u32[]{:S(2)}, u32[]{:S(2)}) collective-permute-start(f32[8,64,256]{2,1,0:T(8,128)} %param.13), channel_id=1, source_target_pairs={{0,224},{32,0},{64,32},{96,64},{128,96},{160,128},{192,160},{224,1... | collective-permute-start | bytes 1572872 | tf_op jit(solution)/shard_map/ppermute | solution.py:15
  6.7 1.1 concatenate.11
  7.9 69.8 %while.32 = (s32[]{:T(128)}, f32[16]{0:T(128)S(1)}, s32[16]{0:T(128)S(1)}, f32[16,64,256]{2,1,0:T(8,128)S(1)}, f32[8,64,256]{2,1,0:T(8,128)S(1)}, /*index=5*/s32[]{:T(128)}, s32[]{:T(128)}, s32[]{:T(128)}) while((s32[]{:T(128)}, f32[16]{0:T(128)S(1)}, s32[16]{0:T(128)S(1)}, f32[16,64,256]{2,1,0:T(8,128)S(1)}, f32[8,64,256]{2,1,0:T(8,128)S(1)}, ...), condition=%wide.region_8.9_spmd, body=%wide.region_6.8_spmd.sunk | while | flops 262148 | bytes 1048727 | solution.py:52
  10.6 0.8 multiply_reduce_fusion.11
  15.0 0.8 multiply_reduce_fusion.11
  19.4 0.8 multiply_reduce_fusion.11
  23.7 0.8 multiply_reduce_fusion.11
  28.1 0.8 multiply_reduce_fusion.11
  32.5 0.8 multiply_reduce_fusion.11
  36.8 0.8 multiply_reduce_fusion.11
  41.2 0.8 multiply_reduce_fusion.11
  45.5 0.8 multiply_reduce_fusion.11
  49.9 0.8 multiply_reduce_fusion.11
  54.3 0.8 multiply_reduce_fusion.11
  58.6 0.8 multiply_reduce_fusion.11
  63.0 0.8 multiply_reduce_fusion.11
  67.4 0.8 multiply_reduce_fusion.11
  71.7 0.8 multiply_reduce_fusion.11
  76.1 0.8 multiply_reduce_fusion.11
  80.1 2.0 pad_maximum_fusion.4
  82.0 6.2 %collective-permute-start.1 = (f32[8,64,256]{2,1,0:T(8,128)S(1)}, f32[8,64,256]{2,1,0:T(8,128)}, u32[]{:S(2)}, u32[]{:S(2)}) collective-permute-start(f32[8,64,256]{2,1,0:T(8,128)S(1)} %collective-permute-done), channel_id=1, source_target_pairs={{0,31},{1,0},{2,1},{3,2},{4,3},{5,4},{6,5},{7,6},{8,7},{9,8},{10,9... | collective-permute-start | bytes 1572872 | tf_op jit(solution)/shard_map/ppermute | solution.py:15
  88.3 1.2 pad_maximum_fusion.1
  89.5 70.9 %while.31 = (s32[]{:T(128)}, f32[16]{0:T(128)S(1)}, f32[8,64,512]{2,1,0:T(8,128)S(1)}, s32[16]{0:T(128)S(1)}, s32[]{:T(128)}, /*index=5*/s32[]{:T(128)}, s32[]{:T(128)}) while((s32[]{:T(128)}, f32[16]{0:T(128)S(1)}, f32[8,64,512]{2,1,0:T(8,128)S(1)}, s32[16]{0:T(128)S(1)}, s32[]{:T(128)}, /*index=5*/s32[]{:T(128)}, s32[]{:T(128)}) %tuple.58), condition=%wide.region_5.6_spmd, body=%wide.region_3.5_spmd.sunk | while | flops 262148 | bytes 1048719 | solution.py:32
  92.2 0.9 multiply_reduce_fusion.10
  96.6 0.9 multiply_reduce_fusion.10
  101.1 0.9 multiply_reduce_fusion.10
  105.5 0.9 multiply_reduce_fusion.10
  109.9 0.9 multiply_reduce_fusion.10
  114.3 0.9 multiply_reduce_fusion.10
  118.8 0.9 multiply_reduce_fusion.10
  123.2 0.9 multiply_reduce_fusion.10
  127.6 0.9 multiply_reduce_fusion.10
  132.1 0.9 multiply_reduce_fusion.10
  136.5 0.9 multiply_reduce_fusion.10
  140.9 0.9 multiply_reduce_fusion.10
  145.3 0.9 multiply_reduce_fusion.10
  149.8 0.9 multiply_reduce_fusion.10
  154.2 0.9 multiply_reduce_fusion.10
  158.6 0.9 multiply_reduce_fusion.10
  160.3 1.2 pad_maximum_fusion
  161.5 64.5 %while.30 = (s32[]{:T(128)}, f32[16]{0:T(128)S(1)}, f32[8,192,256]{2,1,0:T(8,128)S(1)}, s32[16]{0:T(128)S(1)}, s32[]{:T(128)}, /*index=5*/s32[]{:T(128)}, s32[]{:T(128)}) while((s32[]{:T(128)}, f32[16]{0:T(128)S(1)}, f32[8,192,256]{2,1,0:T(8,128)S(1)}, s32[16]{0:T(128)S(1)}, s32[]{:T(128)}, /*index=5*/s32[]{:T(128)}, s32[]{:T(128)}) %tuple.59), condition=%wide.region_2.3_spmd, body=%wide.region_0.2_spmd.sunk | while | flops 262148 | bytes 1048719 | solution.py:32
  226.0 6.5 %all-reduce.2 = (f32[3,16]{1,0:T(4,128)S(1)}, f32[3]{0:T(128)S(1)}) all-reduce(f32[3,16]{1,0:T(4,128)S(1)} %pad_maximum_fusion.2, f32[3]{0:T(128)S(1)} %pad_maximum_fusion.4), channel_id=1, replica_groups=mesh['gy_0'=4,'gy_1'=2,'gx_0'=2,'gx_1'=8,'gx_2'=2] {'gy_0'}, use_global_device_ids=true, to_apply=%region_9.10 | all-reduce | flops 51 | bytes 408 | tf_op jit(solution)/shard_map/psum | solution.py:20
  232.5 5.3 %all-reduce.5 = (f32[3,16]{1,0:T(4,128)S(1)}, f32[3]{0:T(128)S(1)}) all-reduce(f32[3,16]{1,0:T(4,128)S(1)} %get-tuple-element.107, f32[3]{0:T(128)S(1)} %get-tuple-element.108), channel_id=1, replica_groups=mesh['gy_0'=4,'gy_1'=2,'gx_0'=2,'gx_1'=8,'gx_2'=2] {'gy_1'}, use_global_device_ids=true, to_apply=%region_10.11 | all-reduce | flops 51 | bytes 408 | tf_op jit(solution)/shard_map/psum | solution.py:20
  237.8 3.8 %all-reduce.4 = (f32[3,16]{1,0:T(4,128)S(1)}, f32[3]{0:T(128)S(1)}) all-reduce(f32[3,16]{1,0:T(4,128)S(1)} %get-tuple-element.113, f32[3]{0:T(128)S(1)} %get-tuple-element.114), channel_id=1, replica_groups=mesh['gy_0'=4,'gy_1'=2,'gx_0'=2,'gx_1'=8,'gx_2'=2] {'gx_0'}, use_global_device_ids=true, to_apply=%region_11.12 | all-reduce | flops 51 | bytes 408 | tf_op jit(solution)/shard_map/psum | solution.py:20
  241.5 10.7 %all-reduce.1 = (f32[3,16]{1,0:T(4,128)S(1)}, f32[3]{0:T(128)S(1)}) all-reduce(f32[3,16]{1,0:T(4,128)S(1)} %get-tuple-element.111, f32[3]{0:T(128)S(1)} %get-tuple-element.112), channel_id=1, replica_groups=mesh['gy_0'=4,'gy_1'=2,'gx_0'=2,'gx_1'=8,'gx_2'=2] {'gx_1'}, use_global_device_ids=true, to_apply=%region_12.13 | all-reduce | flops 51 | bytes 408 | tf_op jit(solution)/shard_map/psum | solution.py:20
  252.3 10.6 %all-reduce.3 = (f32[3,16]{1,0:T(4,128)S(1)}, f32[3]{0:T(128)S(1)}) all-reduce(f32[3,16]{1,0:T(4,128)S(1)} %get-tuple-element.105, f32[3]{0:T(128)S(1)} %get-tuple-element.106), channel_id=1, replica_groups=mesh['gy_0'=4,'gy_1'=2,'gx_0'=2,'gx_1'=8,'gx_2'=2] {'gx_2'}, use_global_device_ids=true, to_apply=%region_13.14 | all-reduce | flops 51 | bytes 408 | tf_op jit(solution)/shard_map/psum | solution.py:20
  264.2 1.2 slice_divide_fusion.1
  (137 shorter events, 84.6 us)
Async XLA Ops:
  0.0 7.8 %copy-start = (f32[8,64,256]{2,1,0:T(8,128)S(1)}, f32[8,64,256]{2,1,0:T(8,128)}, u32[]{:S(2)}) copy-start(f32[8,64,256]{2,1,0:T(8,128)} %param.14) | copy-start | bytes 1572868
  0.0 7.8 %copy-start.3 = (s32[16]{0:T(128)S(1)}, s32[16]{0:T(128)}, u32[]{:S(2)}) copy-start(s32[16]{0:T(128)} %param.17) | copy-start | bytes 196
  0.0 82.0 %collective-permute-start = (f32[8,64,256]{2,1,0:T(8,128)}, f32[8,64,256]{2,1,0:T(8,128)S(1)}, u32[]{:S(2)}, u32[]{:S(2)}) collective-permute-start(f32[8,64,256]{2,1,0:T(8,128)} %param.12), channel_id=1, source_target_pairs={{0,31},{1,0},{2,1},{3,2},{4,3},{5,4},{6,5},{7,6},{8,7},{9,8},{10,9... | collective-permute-start | bytes 1572872 | tf_op jit(solution)/shard_map/ppermute | solution.py:15
  3.2 85.1 %collective-permute-start.2 = (f32[8,64,256]{2,1,0:T(8,128)}, f32[8,64,256]{2,1,0:T(8,128)}, u32[]{:S(2)}, u32[]{:S(2)}) collective-permute-start(f32[8,64,256]{2,1,0:T(8,128)} %param.13), channel_id=1, source_target_pairs={{0,224},{32,0},{64,32},{96,64},{128,96},{160,128},{192,160},{224,1... | collective-permute-start | bytes 1572872 | tf_op jit(solution)/shard_map/ppermute | solution.py:15
  7.9 69.9 %copy-start.1 = (f32[8,64,256]{2,1,0:T(8,128)S(1)}, f32[8,64,256]{2,1,0:T(8,128)}, u32[]{:S(2)}) copy-start(f32[8,64,256]{2,1,0:T(8,128)} %param.13) | copy-start | bytes 1572868
  7.9 71.4 %copy-start.2 = (f32[8,64,256]{2,1,0:T(8,128)S(1)}, f32[8,64,256]{2,1,0:T(8,128)}, u32[]{:S(2)}) copy-start(f32[8,64,256]{2,1,0:T(8,128)} %param.12) | copy-start | bytes 1572868
  78.4 11.0 %copy-start.4 = (s32[16]{0:T(128)S(1)}, s32[16]{0:T(128)}, u32[]{:S(2)}) copy-start(s32[16]{0:T(128)} %param.16) | copy-start | bytes 196
  82.0 78.3 %collective-permute-start.1 = (f32[8,64,256]{2,1,0:T(8,128)S(1)}, f32[8,64,256]{2,1,0:T(8,128)}, u32[]{:S(2)}, u32[]{:S(2)}) collective-permute-start(f32[8,64,256]{2,1,0:T(8,128)S(1)} %collective-permute-done), channel_id=1, source_target_pairs={{0,31},{1,0},{2,1},{3,2},{4,3},{5,4},{6,5},{7,6},{8,7},{9,8},{10,9... | collective-permute-start | bytes 1572872 | tf_op jit(solution)/shard_map/ppermute | solution.py:15
  160.3 1.2 copy-start.5
where the time goes:
time: 268 us; the launch traced here: 266 us
  loops' own time  97.6 us (36%)
  local copies, waits for them, and re-layouts  70.1 us (26%)
  other arithmetic  48.5 us (18%)
  blocking collectives  36.8 us (14%)
  starting transfers between devices  12.9 us (5%)
    another operation x2, loops' own time, lag_sums(): return lax.map(one_lag, (leading, lag_values))  64.4 us
    dynamic_update_slice x48, local copies, waits for them, and re-layouts, lag_sums(): return lax.map(one_lag, (leading, lag_values))  37.7 us
    psum x5, blocking collectives, by_axis(): x = lax.psum(x, axis)  36.8 us
    another operation x1, loops' own time, local(): sums_z = lax.map(along_z, sep_z)  33.3 us
    dynamic_slice x48, local copies, waits for them, and re-layouts, lag_sums(): return lax.map(one_lag, (leading, lag_values))  30.6 us
    reduce_sum x32, other arithmetic, one_lag(): return jnp.sum(head * tail)  26.2 us
    reduce_sum x16, other arithmetic, along_z(): return jnp.sum(w_field * shifted)  13.1 us
    ppermute x3, starting transfers between devices, from_behind(): return lax.ppermute(value, axis, pairs)  12.9 us
  transfers between devices with their start and end apart: 3, of which 0 were waited for; matrix products, arithmetic and copies ran while one was open for 30% of the time, Pallas kernels for 0%

commit v1 on v0

--- a/solution.py
+++ b/solution.py
@@ -17,7 +17,7 @@
 
 def by_axis(x, axes):
     for axis in axes:
-        x = lax.psum(x, axis)
+        x = jnp.sum(lax.all_gather(x, axis), axis=0)
     return x
 
 

time: 268 us -> 313 us (1.17)
  blocking collectives: 36.8 us -> 87.3 us
  loops' own time: 97.6 us -> 91.2 us
  starting transfers between devices: 12.9 us -> 7.11 us
  between operations: 0.12 us -> 3.44 us
    all_gather x0 -> x5, blocking collectives: none -> 44.6 us  [by_axis(): x = jnp.sum(lax.all_gather(x, axis), axis=0)]
    unnamed x0 -> x5, blocking collectives: none -> 42.7 us
    psum x5 -> x0, blocking collectives: 36.8 us -> none  [by_axis(): x = lax.psum(x, axis)]
    another operation x2, loops' own time: 64.4 us -> 58 us  [lag_sums(): return lax.map(one_lag, (leading, lag_values))]
    ppermute x3, starting transfers between devices: 12.9 us -> 7.11 us  [from_behind(): return lax.ppermute(value, axis, pairs)]
    unnamed x12 -> x36, local copies, waits for them, and re-layouts: 0.03 us -> 3.94 us
  transfers between devices with their start and end apart: 3 -> 3, of which waited for: 0 -> 0; matrix products, arithmetic and copies ran while one was open for 30% -> 27% of each run, Pallas kernels for 0% -> 0%
where the time goes in v1:
time: 313 us; the launch traced here: 308 us
  loops' own time  91.2 us (29%)
  blocking collectives  87.3 us (28%)
  local copies, waits for them, and re-layouts  69.8 us (22%)
  other arithmetic  49.4 us (16%)
  starting transfers between devices  7.11 us (2%)
  between operations  3.44 us (1%)
    another operation x2, loops' own time, lag_sums(): return lax.map(one_lag, (leading, lag_values))  58 us
    all_gather x5, blocking collectives, by_axis(): x = jnp.sum(lax.all_gather(x, axis), axis=0)  44.6 us
    unnamed x5, blocking collectives  42.7 us
    dynamic_update_slice x48, local copies, waits for them, and re-layouts, lag_sums(): return lax.map(one_lag, (leading, lag_values))  35.6 us
    another operation x1, loops' own time, local(): sums_z = lax.map(along_z, sep_z)  33.2 us
    dynamic_slice x48, local copies, waits for them, and re-layouts, lag_sums(): return lax.map(one_lag, (leading, lag_values))  29.1 us
    reduce_sum x32, other arithmetic, one_lag(): return jnp.sum(head * tail)  24.8 us
    reduce_sum x16, other arithmetic, along_z(): return jnp.sum(w_field * shifted)  13.1 us
  transfers between devices with their start and end apart: 3, of which 0 were waited for; matrix products, arithmetic and copies ran while one was open for 27% of the time, Pallas kernels for 0%

profile of v1, /device:TPU:1, one launch (start us, length us, event | category | flops | bytes accessed | tf_op | source)
XLA Modules:
  0.0 308.3 jit_solution(1507923410366247618)
XLA Ops:
  0.0 3.3 %collective-permute-start = (f32[8,64,256]{2,1,0:T(8,128)}, f32[8,64,256]{2,1,0:T(8,128)S(1)}, u32[]{:S(2)}, u32[]{:S(2)}) collective-permute-start(f32[8,64,256]{2,1,0:T(8,128)} %param.12), channel_id=1, source_target_pairs={{0,31},{1,0},{2,1},{3,2},{4,3},{5,4},{6,5},{7,6},{8,7},{9,8},{10,9... | collective-permute-start | bytes 1572872 | tf_op jit(solution)/shard_map/ppermute | solution.py:15
  3.3 3.5 %collective-permute-start.2 = (f32[8,64,256]{2,1,0:T(8,128)}, f32[8,64,256]{2,1,0:T(8,128)S(1)}, u32[]{:S(2)}, u32[]{:S(2)}) collective-permute-start(f32[8,64,256]{2,1,0:T(8,128)} %param.13), channel_id=1, source_target_pairs={{0,224},{32,0},{64,32},{96,64},{128,96},{160,128},{192,160},{224,1... | collective-permute-start | bytes 1572872 | tf_op jit(solution)/shard_map/ppermute | solution.py:15
  6.8 1.8 multiply_reduce_fusion.5
  8.6 1.8 multiply_reduce_fusion.4
  10.4 1.9 multiply_reduce_fusion.3
  13.5 2.0 maximum_dynamic-update-slice_fusion
  15.6 6.5 %all-reduce.1 = f32[12]{0:T(128)S(1)} all-reduce(f32[12]{0:T(128)S(1)} %maximum_dynamic-update-slice_fusion), channel_id=7, replica_groups=mesh['gy_0'=4,'gy_1'=2,'gx_0'=2,'gx_1'=8,'gx_2'=2] {'gy_0'}, use_global_device_ids=true, to_apply=%add.1 | all-reduce | flops 12 | bytes 96
  23.7 5.3 %all-reduce.2 = f32[6]{0:T(128)S(1)} all-reduce(f32[6]{0:T(128)S(1)} %dynamic-update-slice.1), channel_id=8, replica_groups=mesh['gy_0'=4,'gy_1'=2,'gx_0'=2,'gx_1'=8,'gx_2'=2] {'gy_1'}, use_global_device_ids=true, to_apply=%add.2 | all-reduce | flops 6 | bytes 48
  30.5 3.8 %all-reduce.3 = f32[6]{0:T(128)S(1)} all-reduce(f32[6]{0:T(128)S(1)} %dynamic-update-slice.2), channel_id=9, replica_groups=mesh['gy_0'=4,'gy_1'=2,'gx_0'=2,'gx_1'=8,'gx_2'=2] {'gx_0'}, use_global_device_ids=true, to_apply=%add.3 | all-reduce | flops 6 | bytes 48
  35.9 16.7 %all-reduce.4 = f32[24]{0:T(128)S(1)} all-reduce(f32[24]{0:T(128)S(1)} %dynamic-update-slice.3), channel_id=10, replica_groups=mesh['gy_0'=4,'gy_1'=2,'gx_0'=2,'gx_1'=8,'gx_2'=2] {'gx_1'}, use_global_device_ids=true, to_apply=%add.4 | all-reduce | flops 24 | bytes 192
  54.3 69.7 %while.32 = (s32[]{:T(128)}, f32[16]{0:T(128)S(1)}, s32[16]{0:T(128)S(1)}, f32[16,64,256]{2,1,0:T(8,128)S(1)}, f32[8,64,256]{2,1,0:T(8,128)S(1)}, /*index=5*/s32[]{:T(128)}, s32[]{:T(128)}, s32[]{:T(128)}) while((s32[]{:T(128)}, f32[16]{0:T(128)S(1)}, s32[16]{0:T(128)S(1)}, f32[16,64,256]{2,1,0:T(8,128)S(1)}, f32[8,64,256]{2,1,0:T(8,128)S(1)}, ...), condition=%wide.region_8.9_spmd, body=%wide.region_6.8_spmd.sunk | while | flops 262148 | bytes 1048727 | solution.py:52
  57.1 0.8 multiply_reduce_fusion.11
  61.4 0.8 multiply_reduce_fusion.11
  65.8 0.8 multiply_reduce_fusion.11
  70.1 0.8 multiply_reduce_fusion.11
  74.5 0.8 multiply_reduce_fusion.11
  78.8 0.8 multiply_reduce_fusion.11
  83.2 0.8 multiply_reduce_fusion.11
  87.6 0.8 multiply_reduce_fusion.11
  91.9 0.8 multiply_reduce_fusion.11
  96.3 0.8 multiply_reduce_fusion.11
  100.6 0.8 multiply_reduce_fusion.11
  105.0 0.8 multiply_reduce_fusion.11
  109.3 0.8 multiply_reduce_fusion.11
  113.7 0.8 multiply_reduce_fusion.11
  118.0 0.8 multiply_reduce_fusion.11
  122.4 0.8 multiply_reduce_fusion.11
  124.0 10.5 %all-reduce.5 = f32[6]{0:T(128)S(1)} all-reduce(f32[6]{0:T(128)S(1)} %dynamic-update-slice.4), channel_id=11, replica_groups=mesh['gy_0'=4,'gy_1'=2,'gx_0'=2,'gx_1'=8,'gx_2'=2] {'gx_2'}, use_global_device_ids=true, to_apply=%add.5 | all-reduce | flops 6 | bytes 48
  135.8 59.6 %while.31 = (s32[]{:T(128)}, f32[16]{0:T(128)S(1)}, f32[8,64,512]{2,1,0:T(8,128)S(1)}, s32[16]{0:T(128)S(1)}, s32[]{:T(128)}, /*index=5*/s32[]{:T(128)}, s32[]{:T(128)}) while((s32[]{:T(128)}, f32[16]{0:T(128)S(1)}, f32[8,64,512]{2,1,0:T(8,128)S(1)}, s32[16]{0:T(128)S(1)}, s32[]{:T(128)}, /*index=5*/s32[]{:T(128)}, s32[]{:T(128)}) %tuple.58), condition=%wide.region_5.6_spmd, body=%wide.region_3.5_spmd.sunk | while | flops 262148 | bytes 1048719 | solution.py:32
  138.0 0.8 multiply_reduce_fusion.10
  141.8 0.8 multiply_reduce_fusion.10
  145.5 0.8 multiply_reduce_fusion.10
  149.2 0.8 multiply_reduce_fusion.10
  160.4 0.8 multiply_reduce_fusion.10
  164.1 0.8 multiply_reduce_fusion.10
  167.8 0.8 multiply_reduce_fusion.10
  171.6 0.8 multiply_reduce_fusion.10
  179.0 0.8 multiply_reduce_fusion.10
  186.5 0.8 multiply_reduce_fusion.10
  190.2 0.8 multiply_reduce_fusion.10
  195.4 1.2 pad_maximum_fusion
  196.6 64.5 %while.30 = (s32[]{:T(128)}, f32[16]{0:T(128)S(1)}, f32[8,192,256]{2,1,0:T(8,128)S(1)}, s32[16]{0:T(128)S(1)}, s32[]{:T(128)}, /*index=5*/s32[]{:T(128)}, s32[]{:T(128)}) while((s32[]{:T(128)}, f32[16]{0:T(128)S(1)}, f32[8,192,256]{2,1,0:T(8,128)S(1)}, s32[16]{0:T(128)S(1)}, s32[]{:T(128)}, /*index=5*/s32[]{:T(128)}, s32[]{:T(128)}) %tuple.59), condition=%wide.region_2.3_spmd, body=%wide.region_0.2_spmd.sunk | while | flops 262148 | bytes 1048719 | solution.py:32
  261.1 8.1 %all-gather.10 = f32[4,3,16]{2,1,0:T(4,128)S(1)} all-gather(f32[1,3,16]{2,1,0:T(4,128)S(1)} %maximum_bitcast_fusion), channel_id=2, replica_groups=mesh['gy_0'=4,'gy_1'=2,'gx_0'=2,'gx_1'=8,'gx_2'=2] {'gy_0'}, dimensions={0}, use_global_device_ids=true | all-gather | bytes 960 | tf_op jit(solution)/shard_map/all_gather | solution.py:20
  269.3 4.7 %all-gather.11 = f32[2,3,16]{2,1,0:T(4,128)S(1)} all-gather(f32[1,3,16]{2,1,0:T(4,128)S(1)} %bitcast.47), channel_id=3, replica_groups=mesh['gy_0'=4,'gy_1'=2,'gx_0'=2,'gx_1'=8,'gx_2'=2] {'gy_1'}, dimensions={0}, use_global_device_ids=true | all-gather | bytes 576 | tf_op jit(solution)/shard_map/all_gather | solution.py:20
  274.0 3.2 %all-gather.12 = f32[2,3,16]{2,1,0:T(4,128)S(1)} all-gather(f32[1,3,16]{2,1,0:T(4,128)S(1)} %bitcast.45), channel_id=4, replica_groups=mesh['gy_0'=4,'gy_1'=2,'gx_0'=2,'gx_1'=8,'gx_2'=2] {'gx_0'}, dimensions={0}, use_global_device_ids=true | all-gather | bytes 576 | tf_op jit(solution)/shard_map/all_gather | solution.py:20
  277.2 15.6 %all-gather.13 = f32[8,3,16]{2,1,0:T(4,128)S(1)} all-gather(f32[1,3,16]{2,1,0:T(4,128)S(1)} %bitcast.46), channel_id=5, replica_groups=mesh['gy_0'=4,'gy_1'=2,'gx_0'=2,'gx_1'=8,'gx_2'=2] {'gx_1'}, dimensions={0}, use_global_device_ids=true | all-gather | bytes 1728 | tf_op jit(solution)/shard_map/all_gather | solution.py:20
  292.8 13.0 %all-gather.14 = f32[2,3,16]{2,1,0:T(4,128)S(1)} all-gather(f32[1,3,16]{2,1,0:T(4,128)S(1)} %bitcast.44), channel_id=6, replica_groups=mesh['gy_0'=4,'gy_1'=2,'gx_0'=2,'gx_1'=8,'gx_2'=2] {'gx_2'}, dimensions={0}, use_global_device_ids=true | all-gather | bytes 576 | tf_op jit(solution)/shard_map/all_gather | solution.py:20
  306.4 1.3 slice_divide_fusion.1
  (181 shorter events, 87.6 us)
Async XLA Ops:
  0.0 12.3 %copy-start.10 = (u32[256]{0:T(256)S(1)}, u32[256]{0:T(256)}, u32[]{:S(2)}) copy-start(u32[256]{0:T(256)} %constant.46) | copy-start | bytes 3076
  0.0 22.2 %copy-start.9 = (u32[256]{0:T(256)S(1)}, u32[256]{0:T(256)}, u32[]{:S(2)}) copy-start(u32[256]{0:T(256)} %constant.51) | copy-start | bytes 3076
  0.0 29.0 %copy-start.8 = (u32[256]{0:T(256)S(1)}, u32[256]{0:T(256)}, u32[]{:S(2)}) copy-start(u32[256]{0:T(256)} %constant.56) | copy-start | bytes 3076
  0.0 34.4 %copy-start.7 = (u32[256]{0:T(256)S(1)}, u32[256]{0:T(256)}, u32[]{:S(2)}) copy-start(u32[256]{0:T(256)} %constant.61) | copy-start | bytes 3076
  0.0 52.7 %copy-start.6 = (u32[256]{0:T(256)S(1)}, u32[256]{0:T(256)}, u32[]{:S(2)}) copy-start(u32[256]{0:T(256)} %constant.66) | copy-start | bytes 3076
  0.0 53.9 %copy-start = (f32[8,64,256]{2,1,0:T(8,128)S(1)}, f32[8,64,256]{2,1,0:T(8,128)}, u32[]{:S(2)}) copy-start(f32[8,64,256]{2,1,0:T(8,128)} %param.14) | copy-start | bytes 1572868
  0.0 135.2 %collective-permute-start = (f32[8,64,256]{2,1,0:T(8,128)}, f32[8,64,256]{2,1,0:T(8,128)S(1)}, u32[]{:S(2)}, u32[]{:S(2)}) collective-permute-start(f32[8,64,256]{2,1,0:T(8,128)} %param.12), channel_id=1, source_target_pairs={{0,31},{1,0},{2,1},{3,2},{4,3},{5,4},{6,5},{7,6},{8,7},{9,8},{10,9... | collective-permute-start | bytes 1572872 | tf_op jit(solution)/shard_map/ppermute | solution.py:15
  3.3 132.3 %collective-permute-start.2 = (f32[8,64,256]{2,1,0:T(8,128)}, f32[8,64,256]{2,1,0:T(8,128)S(1)}, u32[]{:S(2)}, u32[]{:S(2)}) collective-permute-start(f32[8,64,256]{2,1,0:T(8,128)} %param.13), channel_id=1, source_target_pairs={{0,224},{32,0},{64,32},{96,64},{128,96},{160,128},{192,160},{224,1... | collective-permute-start | bytes 1572872 | tf_op jit(solution)/shard_map/ppermute | solution.py:15
  6.8 47.5 %copy-start.3 = (s32[16]{0:T(128)S(1)}, s32[16]{0:T(128)}, u32[]{:S(2)}) copy-start(s32[16]{0:T(128)} %param.17) | copy-start | bytes 196
  54.3 81.3 %copy-start.1 = (f32[8,64,256]{2,1,0:T(8,128)S(1)}, f32[8,64,256]{2,1,0:T(8,128)}, u32[]{:S(2)}) copy-start(f32[8,64,256]{2,1,0:T(8,128)} %param.13) | copy-start | bytes 1572868
  124.0 11.7 %copy-start.4 = (s32[16]{0:T(128)S(1)}, s32[16]{0:T(128)}, u32[]{:S(2)}) copy-start(s32[16]{0:T(128)} %param.16) | copy-start | bytes 196
  135.3 60.1 %collective-permute-start.1 = (f32[8,64,256]{2,1,0:T(8,128)S(1)}, f32[8,64,256]{2,1,0:T(8,128)}, u32[]{:S(2)}, u32[]{:S(2)}) collective-permute-start(f32[8,64,256]{2,1,0:T(8,128)S(1)} %collective-permute-done), channel_id=1, source_target_pairs={{0,31},{1,0},{2,1},{3,2},{4,3},{5,4},{6,5},{7,6},{8,7},{9,8},{10,9... | collective-permute-start | bytes 1572872 | tf_op jit(solution)/shard_map/ppermute | solution.py:15
  135.8 59.6 %copy-start.2 = (f32[8,64,256]{2,1,0:T(8,128)S(1)}, f32[8,64,256]{2,1,0:T(8,128)}, u32[]{:S(2)}) copy-start(f32[8,64,256]{2,1,0:T(8,128)} %param.12) | copy-start | bytes 1572868
  195.4 1.2 copy-start.5
